TPU v7x, 256 devices: a 2x2x32 block of a 4x8x32 slice. The times are simulated.
256 devices in a mesh: trait: 4 (over x, y), ppl: 64 (over z, core).
Axes of the slice: x: 2, y: 2, z: 32, core: 2. Of those that a mesh axis runs over, the one named last changes fastest.
The devices are a block of a 4x8x32 slice.
Arguments:
- genotypes: bfloat16 [65536, 4096], P(('trait', 'ppl')), parts along dimension 0
- residual: float32 [128, 16384], P('trait', 'ppl'), parts along dimension 0, may hold values from -36 to 36
- noise_people: float32 [128, 16384], P('trait', 'ppl'), parts along dimension 0, may hold values from -6 to 6
- noise_coef: float32 [128, 4096], P('trait'), parts along dimension 0, may hold values from -6 to 6
- coef_all: float32 [128, 8192], P('trait'), parts along dimension 0, may hold values from -0.06 to 0.06
- block_index: int32 [4], P('trait'), parts along dimension 0, may hold values from 0 to 1
- prior_prec: float32 [128], P('trait'), parts along dimension 0, may hold values from 82 to 410
- sigma2_old: float32 [128], P('trait'), parts along dimension 0, may hold values from 0.5 to 2
- gamma_draw: float32 [128], P('trait'), parts along dimension 0, may hold values from 0.8 to 1.25
- valid_counts: int32 [256], P('trait'), parts along dimension 0, may hold values from 128 to 256, as said below
Outputs:
- coef_new: float32 [128, 8192], P('trait'), parts along dimension 0
- residual_new: float32 [128, 16384], P('trait', 'ppl'), parts along dimension 0
- sigma2_new: float32 [128], P('trait'), parts along dimension 0
There are 4 independent parts, one for each index of `trait`. A program takes and returns all parts, laid end to end along the dimension named above; each array names one. Nothing has to cross between parts.
Inputs may be any that keep to these rules, and one draw needn't show every extreme that they name: `valid_counts`: each entry counts the people present in one device's 256 slots; they fill the lowest slots, and some entry equals 256.
All inputs are finite; a program needn't handle non-finite values.
Results may differ from a plain program's by a relative error of at most 0.0049.
Values may be sent and summed in bfloat16 or wider, within the bound.
A program may use at most 64 MiB of HBM per device.

v0:
```python
import jax
import jax.numpy as jnp
from jax import lax
from jax.sharding import PartitionSpec as P

ITERS = 4


PRIOR_DOF = 4.0
PRIOR_SCALE = 0.5
CONTRACT = (((1,), (1,)), ((), ()))


def sent_to_all(shard, axis):
    copies = jnp.broadcast_to(shard, (lax.axis_size(axis), *shard.shape))
    return lax.all_to_all(copies, axis, split_axis=0, concat_axis=0, tiled=True)


def over_copies(shard, axis):
    everything = sent_to_all(shard, axis)
    return jnp.sum(everything, axis=0)


def in_blocks(shard, dim, devices):
    lengths = shard.shape
    tiles = shard.reshape(*lengths[:dim], devices, lengths[dim] // devices, *lengths[dim + 1 :])
    return jnp.moveaxis(tiles, dim, 0)


def sent_and_summed(shard, axis, dim):
    tiles = in_blocks(shard, dim, lax.axis_size(axis))
    arrived = lax.all_to_all(tiles, axis, split_axis=0, concat_axis=0, tiled=True)
    return arrived.sum(axis=0)


def joined_along(tiles, dim):
    lengths = list(tiles.shape[1:])
    lengths[dim] *= tiles.shape[0]
    return jnp.moveaxis(tiles, 0, dim).reshape(lengths)


def gather_directly(shard, axis, dim):
    return joined_along(sent_to_all(shard, axis), dim)


def sum_at_owner(shard, axis, dim):
    devices = lax.axis_size(axis)
    tiles = lax.all_to_all(in_blocks(shard, dim, devices), axis, 0, 0, tiled=True)
    return jnp.sum(tiles.astype(jnp.float32), axis=0)


def norm_total(search):
    return over_copies(jnp.sum(search * search, axis=1), "ppl")


def per_device(
    genotypes,
    residual,
    noise_people,
    noise_coef,
    coef_all,
    block_index,
    prior_prec,
    sigma2_old,
    gamma_draw,
    valid_counts,
):
    row_count = genotypes.shape[0]
    batch_width = genotypes.shape[1]
    my_shard = lax.axis_index("ppl")
    person_mask = (jnp.arange(row_count) < valid_counts[my_shard]).astype(jnp.float32)[None, :]
    first_col = block_index[0] * batch_width
    old_coef = lax.dynamic_slice_in_dim(coef_all, first_col, batch_width, 1)
    fitted_old = lax.dot_general(
        old_coef.astype(jnp.bfloat16), genotypes, CONTRACT, preferred_element_type=jnp.float32
    )
    partial_res = person_mask * (residual + fitted_old)
    noise_var = sigma2_old[:, None]
    ridge = prior_prec[:, None]
    target = (person_mask * (partial_res + jnp.sqrt(noise_var) * noise_people)).astype(jnp.bfloat16)
    data_part = jnp.dot(target, genotypes, preferred_element_type=jnp.float32)
    fitted = jnp.zeros_like(partial_res)
    share_width = batch_width // lax.axis_size("ppl")
    offset = my_shard * share_width
    own_noise = lax.dynamic_slice_in_dim(noise_coef, offset, share_width, 1)
    rhs = sent_and_summed(data_part, "ppl", 1) / noise_var + jnp.sqrt(ridge) * own_noise
    coef_share = jnp.zeros_like(rhs)
    search = rhs
    direction = rhs
    norm_now = norm_total(search)
    for number in range(ITERS):
        dir_low = direction.astype(jnp.bfloat16)
        dir_full = lax.optimization_barrier(dir_low).astype(jnp.float32)
        image = person_mask * lax.dot_general(
            gather_directly(dir_low, "ppl", 1),
            genotypes,
            CONTRACT,
            preferred_element_type=jnp.float32,
        )
        local_sum = jnp.dot(
            image.astype(jnp.bfloat16), genotypes, preferred_element_type=jnp.float32
        )
        applied = (
            sum_at_owner(local_sum.astype(jnp.bfloat16), "ppl", 1) / noise_var + ridge * dir_full
        )
        curv_sum = over_copies(jnp.sum(dir_full * applied, axis=1), "ppl")
        step_size = norm_now / curv_sum
        coef_share = coef_share + step_size[:, None] * dir_full
        fitted = fitted + step_size[:, None] * image
        search = search - step_size[:, None] * applied
        if number < ITERS - 1:
            norm_next = norm_total(search)
            direction = search + (norm_next / norm_now)[:, None] * direction
            norm_now = norm_next
    batch_coef = lax.all_gather(coef_share, "ppl", axis=1, tiled=True)
    residual_new = partial_res - fitted
    squares = over_copies(jnp.sum(residual_new * residual_new, axis=1), "ppl")
    present = jnp.sum(valid_counts).astype(jnp.float32)
    sigma2_new = (squares + PRIOR_DOF * PRIOR_SCALE) / ((present + PRIOR_DOF) * gamma_draw)
    coef_new = lax.dynamic_update_slice_in_dim(coef_all, batch_coef, first_col, 1)
    return (coef_new, residual_new, sigma2_new)


def solution(mesh):
    return jax.shard_map(
        per_device,
        mesh=mesh,
        in_specs=(
            P(("trait", "ppl"), None),
            P("trait", "ppl"),
            P("trait", "ppl"),
            P("trait", None),
            P("trait", None),
            P("trait"),
            P("trait"),
            P("trait"),
            P("trait"),
            P("trait"),
        ),
        out_specs=(P("trait", None), P("trait", "ppl"), P("trait")),
        check_vma=False,
    )
```

profile of v0, /device:TPU:37, one launch (start us, length us, event | category | flops | bytes accessed | tf_op | source)
XLA Modules:
  0.0 820.4 jit_solution(16349355247402962628)
XLA Ops:
  0.7 1.4 copy.85
  2.1 0.7 dynamic_slice.9
  2.7 0.6 compare_convert_fusion
  4.1 0.7 fusion
  4.9 1.3 fusion.13
  6.2 1.5 reshape.117
  7.6 1.6 copy.77
  9.2 2.7 reshape.128
  11.9 34.3 %all-to-all-start = ((f32[64,1,2048]{2,1,0:T(1,128)}), f32[64,1,2048]{2,1,0:T(1,128)S(1)}, u32[]{:S(2)}, u32[]{:S(2)}) async-start(f32[64,1,2048]{2,1,0:T(1,128)} %reshape.128), calls=%async_computation | async-start | bytes 1048576 | tf_op jit(solution)/shard_map/all_to_all | solution.py:32
  46.3 63.9 %all-to-all-done = f32[64,1,2048]{2,1,0:T(1,128)S(1)} async-done(((f32[64,1,2048]{2,1,0:T(1,128)}), f32[64,1,2048]{2,1,0:T(1,128)S(1)}, u32[]{:S(2)}, u32[]{:S(2)}) %all-to-all-start) | async-done | bytes 524320 | tf_op jit(solution)/shard_map/all_to_all | solution.py:32
  110.2 0.5 broadcast.35
  110.8 2.8 reduce.9
  113.5 1.5 reshape.129
  115.1 0.9 multiply_reduce_fusion.4
  116.4 48.2 %all_to_all.99 = bf16[64,2,1024]{2,1,0:T(2,128)(2,1)S(1)} all-to-all(bf16[64,2,1024]{2,1,0:T(2,128)(2,1)S(1)} %reshape.130), channel_id=1, replica_groups=mesh['trait'=4,'ppl'=64] {'ppl'}, dimensions={0} | all-to-all | bytes 524288 | tf_op jit(solution)/shard_map/all_to_all | solution.py:16
  165.6 0.7 convolution_multiply_fusion.3
  166.9 0.5 reshape.119
  167.8 1.0 reshape.132
  168.8 6.0 all-to-all-start.3
  174.8 42.6 %all-to-all-done.3 = bf16[64,2,1024]{2,1,0:T(2,128)(2,1)S(1)} async-done(((bf16[64,2,1024]{2,1,0:T(2,128)(2,1)}), bf16[64,2,1024]{2,1,0:T(2,128)(2,1)S(1)}, u32[]{:S(2)}, u32[]{:S(2)}) %all-to-all-start.3) | async-done | bytes 262176 | tf_op jit(solution)/shard_map/all_to_all | solution.py:48
  217.4 0.6 broadcast_in_dim.26
  218.1 5.5 all-to-all-start.1
  224.3 21.8 %all-to-all-done.1 = f32[64,1,32]{2,1,0:T(1,128)S(1)} async-done(((f32[64,1,32]{2,1,0:T(1,128)}), f32[64,1,32]{2,1,0:T(1,128)S(1)}, u32[]{:S(2)}, u32[]{:S(2)}) %all-to-all-start.1) | async-done | bytes 8224 | tf_op jit(solution)/shard_map/all_to_all | solution.py:16
  246.1 0.6 broadcast_in_dim.28
  246.8 5.9 all-to-all-start.4
  252.7 22.4 %all-to-all-done.4 = f32[64,1,32]{2,1,0:T(1,128)S(1)} async-done(((f32[64,1,32]{2,1,0:T(1,128)}), f32[64,1,32]{2,1,0:T(1,128)S(1)}, u32[]{:S(2)}, u32[]{:S(2)}) %all-to-all-start.4) | async-done | bytes 8224 | tf_op jit(solution)/shard_map/all_to_all | solution.py:16
  275.5 27.9 %all_to_all.100 = f32[64,1,32]{2,1,0:T(1,128)S(1)} all-to-all(f32[64,1,32]{2,1,0:T(1,128)S(1)} %broadcast_in_dim.29), channel_id=1, replica_groups=mesh['trait'=4,'ppl'=64] {'ppl'}, dimensions={0} | all-to-all | bytes 16384 | tf_op jit(solution)/shard_map/all_to_all | solution.py:16
  304.0 47.2 %all_to_all.101 = bf16[64,2,1024]{2,1,0:T(2,128)(2,1)S(1)} all-to-all(bf16[64,2,1024]{2,1,0:T(2,128)(2,1)S(1)} %reshape.134), channel_id=1, replica_groups=mesh['trait'=4,'ppl'=64] {'ppl'}, dimensions={0} | all-to-all | bytes 524288 | tf_op jit(solution)/shard_map/all_to_all | solution.py:16
  352.2 0.7 convolution_multiply_fusion.2
  352.9 0.5 convolution_convert_fusion.2
  353.4 0.5 reshape.121
  354.3 1.0 reshape.136
  355.3 6.0 all-to-all-start.7
  361.4 42.6 %all-to-all-done.7 = bf16[64,2,1024]{2,1,0:T(2,128)(2,1)S(1)} async-done(((bf16[64,2,1024]{2,1,0:T(2,128)(2,1)}), bf16[64,2,1024]{2,1,0:T(2,128)(2,1)S(1)}, u32[]{:S(2)}, u32[]{:S(2)}) %all-to-all-start.7) | async-done | bytes 262176 | tf_op jit(solution)/shard_map/all_to_all | solution.py:48
  404.7 27.6 %all_to_all.102 = f32[64,1,32]{2,1,0:T(1,128)S(1)} all-to-all(f32[64,1,32]{2,1,0:T(1,128)S(1)} %broadcast_in_dim.61), channel_id=1, replica_groups=mesh['trait'=4,'ppl'=64] {'ppl'}, dimensions={0} | all-to-all | bytes 16384 | tf_op jit(solution)/shard_map/all_to_all | solution.py:16
  432.6 27.7 %all_to_all.103 = f32[64,1,32]{2,1,0:T(1,128)S(1)} all-to-all(f32[64,1,32]{2,1,0:T(1,128)S(1)} %broadcast_in_dim.62), channel_id=1, replica_groups=mesh['trait'=4,'ppl'=64] {'ppl'}, dimensions={0} | all-to-all | bytes 16384 | tf_op jit(solution)/shard_map/all_to_all | solution.py:16
  460.9 47.3 %all_to_all.104 = bf16[64,2,1024]{2,1,0:T(2,128)(2,1)S(1)} all-to-all(bf16[64,2,1024]{2,1,0:T(2,128)(2,1)S(1)} %reshape.138), channel_id=1, replica_groups=mesh['trait'=4,'ppl'=64] {'ppl'}, dimensions={0} | all-to-all | bytes 524288 | tf_op jit(solution)/shard_map/all_to_all | solution.py:16
  509.1 0.7 convolution_multiply_fusion.1
  509.9 0.5 convolution_convert_fusion.1
  510.4 0.5 reshape.123
  511.3 1.0 reshape.140
  512.3 6.0 all-to-all-start.11
  518.3 42.6 %all-to-all-done.11 = bf16[64,2,1024]{2,1,0:T(2,128)(2,1)S(1)} async-done(((bf16[64,2,1024]{2,1,0:T(2,128)(2,1)}), bf16[64,2,1024]{2,1,0:T(2,128)(2,1)S(1)}, u32[]{:S(2)}, u32[]{:S(2)}) %all-to-all-start.11) | async-done | bytes 262176 | tf_op jit(solution)/shard_map/all_to_all | solution.py:48
  561.7 27.6 %all_to_all.105 = f32[64,1,32]{2,1,0:T(1,128)S(1)} all-to-all(f32[64,1,32]{2,1,0:T(1,128)S(1)} %broadcast_in_dim.64), channel_id=1, replica_groups=mesh['trait'=4,'ppl'=64] {'ppl'}, dimensions={0} | all-to-all | bytes 16384 | tf_op jit(solution)/shard_map/all_to_all | solution.py:16
  589.6 27.7 %all_to_all.106 = f32[64,1,32]{2,1,0:T(1,128)S(1)} all-to-all(f32[64,1,32]{2,1,0:T(1,128)S(1)} %broadcast_in_dim.65), channel_id=1, replica_groups=mesh['trait'=4,'ppl'=64] {'ppl'}, dimensions={0} | all-to-all | bytes 16384 | tf_op jit(solution)/shard_map/all_to_all | solution.py:16
  617.8 47.3 %all_to_all.107 = bf16[64,2,1024]{2,1,0:T(2,128)(2,1)S(1)} all-to-all(bf16[64,2,1024]{2,1,0:T(2,128)(2,1)S(1)} %reshape.142), channel_id=1, replica_groups=mesh['trait'=4,'ppl'=64] {'ppl'}, dimensions={0} | all-to-all | bytes 524288 | tf_op jit(solution)/shard_map/all_to_all | solution.py:16
  666.1 0.7 convolution_multiply_fusion
  666.9 0.5 convolution_convert_fusion
  667.4 0.5 reshape.125
  668.3 1.0 reshape.144
  669.3 6.0 all-to-all-start.15
  675.3 42.6 %all-to-all-done.15 = bf16[64,2,1024]{2,1,0:T(2,128)(2,1)S(1)} async-done(((bf16[64,2,1024]{2,1,0:T(2,128)(2,1)}), bf16[64,2,1024]{2,1,0:T(2,128)(2,1)S(1)}, u32[]{:S(2)}, u32[]{:S(2)}) %all-to-all-start.15) | async-done | bytes 262176 | tf_op jit(solution)/shard_map/all_to_all | solution.py:48
  718.6 0.6 broadcast_in_dim.67
  719.3 5.5 all-to-all-start.16
  724.8 0.6 reduce_sum.239
  726.1 21.2 %all-to-all-done.16 = f32[64,1,32]{2,1,0:T(1,128)S(1)} async-done(((f32[64,1,32]{2,1,0:T(1,128)}), f32[64,1,32]{2,1,0:T(1,128)S(1)}, u32[]{:S(2)}, u32[]{:S(2)}) %all-to-all-start.16) | async-done | bytes 8224 | tf_op jit(solution)/shard_map/all_to_all | solution.py:16
  747.4 0.8 multiply_reduce_fusion
  748.3 0.6 broadcast_in_dim.68
  748.9 5.9 all-to-all-start.17
  754.9 60.8 %all-gather = f32[64,64,32]{1,2,0:T(8,128)S(1)} all-gather(f32[1,64,32]{1,2,0:T(8,128)S(1)} %fusion.6), channel_id=1, replica_groups=mesh['trait'=4,'ppl'=64] {'ppl'}, dimensions={0}, use_global_device_ids=true | all-gather | bytes 532480 | tf_op jit(solution)/shard_map/all_gather | solution.py:115
  815.7 0.6 copy.61
  816.3 1.1 reshape.127
  817.5 1.9 bitcast_dynamic-update-slice_fusion
  819.4 0.5 multiply_divide_fusion
  (86 shorter events, 11.9 us)
Async XLA Ops:
  0.6 3.4 copy-start
  0.6 3.4 copy-start.3
  0.7 4.2 copy-start.4
  0.7 3.4 copy-start.2
  0.7 1.4 copy-start.7
  2.1 2.8 copy-start.1
  7.6 38.6 %copy-start.5 = (f32[32]{0:T(128)S(1)}, f32[32]{0:T(128)}, u32[]{:S(2)}) copy-start(f32[32]{0:T(128)} %param.16) | copy-start | bytes 388
  11.9 98.3 %all-to-all-start = ((f32[64,1,2048]{2,1,0:T(1,128)}), f32[64,1,2048]{2,1,0:T(1,128)S(1)}, u32[]{:S(2)}, u32[]{:S(2)}) async-start(f32[64,1,2048]{2,1,0:T(1,128)} %reshape.128), calls=%async_computation | async-start | bytes 1048576 | tf_op jit(solution)/shard_map/all_to_all | solution.py:32
  168.8 48.7 %all-to-all-start.3 = ((bf16[64,2,1024]{2,1,0:T(2,128)(2,1)}), bf16[64,2,1024]{2,1,0:T(2,128)(2,1)S(1)}, u32[]{:S(2)}, u32[]{:S(2)}) async-start(bf16[64,2,1024]{2,1,0:T(2,128)(2,1)} %reshape.132), calls=%async_computation.3 | async-start | bytes 524288 | tf_op jit(solution)/shard_map/all_to_all | solution.py:48
  218.1 28.1 %all-to-all-start.1 = ((f32[64,1,32]{2,1,0:T(1,128)}), f32[64,1,32]{2,1,0:T(1,128)S(1)}, u32[]{:S(2)}, u32[]{:S(2)}) async-start(f32[64,1,32]{2,1,0:T(1,128)} %broadcast_in_dim.26), calls=%async_computation.1 | async-start | bytes 65536 | tf_op jit(solution)/shard_map/all_to_all | solution.py:16
  246.8 28.4 %all-to-all-start.4 = ((f32[64,1,32]{2,1,0:T(1,128)}), f32[64,1,32]{2,1,0:T(1,128)S(1)}, u32[]{:S(2)}, u32[]{:S(2)}) async-start(f32[64,1,32]{2,1,0:T(1,128)} %broadcast_in_dim.28), calls=%async_computation.4 | async-start | bytes 65536 | tf_op jit(solution)/shard_map/all_to_all | solution.py:16
  355.3 48.7 %all-to-all-start.7 = ((bf16[64,2,1024]{2,1,0:T(2,128)(2,1)}), bf16[64,2,1024]{2,1,0:T(2,128)(2,1)S(1)}, u32[]{:S(2)}, u32[]{:S(2)}) async-start(bf16[64,2,1024]{2,1,0:T(2,128)(2,1)} %reshape.136), calls=%async_computation.7 | async-start | bytes 524288 | tf_op jit(solution)/shard_map/all_to_all | solution.py:48
  512.3 48.7 %all-to-all-start.11 = ((bf16[64,2,1024]{2,1,0:T(2,128)(2,1)}), bf16[64,2,1024]{2,1,0:T(2,128)(2,1)S(1)}, u32[]{:S(2)}, u32[]{:S(2)}) async-start(bf16[64,2,1024]{2,1,0:T(2,128)(2,1)} %reshape.140), calls=%async_computation.11 | async-start | bytes 524288 | tf_op jit(solution)/shard_map/all_to_all | solution.py:48
  669.3 48.7 %all-to-all-start.15 = ((bf16[64,2,1024]{2,1,0:T(2,128)(2,1)}), bf16[64,2,1024]{2,1,0:T(2,128)(2,1)S(1)}, u32[]{:S(2)}, u32[]{:S(2)}) async-start(bf16[64,2,1024]{2,1,0:T(2,128)(2,1)} %reshape.144), calls=%async_computation.15 | async-start | bytes 524288 | tf_op jit(solution)/shard_map/all_to_all | solution.py:48
  719.3 28.1 %all-to-all-start.16 = ((f32[64,1,32]{2,1,0:T(1,128)}), f32[64,1,32]{2,1,0:T(1,128)S(1)}, u32[]{:S(2)}, u32[]{:S(2)}) async-start(f32[64,1,32]{2,1,0:T(1,128)} %broadcast_in_dim.67), calls=%async_computation.16 | async-start | bytes 65536 | tf_op jit(solution)/shard_map/all_to_all | solution.py:16
  748.9 70.4 %all-to-all-start.17 = ((f32[64,1,32]{2,1,0:T(1,128)}), f32[64,1,32]{2,1,0:T(1,128)S(1)}, u32[]{:S(2)}, u32[]{:S(2)}) async-start(f32[64,1,32]{2,1,0:T(1,128)} %broadcast_in_dim.68), calls=%async_computation.17 | async-start | bytes 65536 | tf_op jit(solution)/shard_map/all_to_all | solution.py:16
  815.7 3.7 copy-start.6
where the time goes:
time: 830 us; the launch traced here: 820 us
  blocking collectives  389 us (47%)
  waiting for transfers between devices  300 us (36%)
  starting transfers between devices  81.4 us (10%)
  local copies, waits for them, and re-layouts  30.5 us (4%)
  other arithmetic  9.41 us (1%)
    all_to_all x9, blocking collectives, sent_to_all(): return lax.all_to_all(copies, axis, split_axis=0, concat_axis=0, tiled=True)  328 us
    all_to_all x4, waiting for transfers between devices, sum_at_owner(): lax.all_to_all(in_blocks(shard, dim, devices), axis, 0, 0, tiled=True)  171 us
    all_to_all x4, waiting for transfers between devices, sent_to_all(): return lax.all_to_all(copies, axis, split_axis=0, concat_axis=0, tiled=True)  65.5 us
    all_to_all x1, waiting for transfers between devices, sent_and_summed(): lax.all_to_all(tiles, axis, split_axis=0, concat_axis=0, tiled=True)  63.9 us
    all_gather x1, blocking collectives, per_device(): batch_coef = lax.all_gather(coef_share, 'ppl', axis=1, tiled=True)  60.8 us
    all_to_all x1, starting transfers between devices, sent_and_summed(): lax.all_to_all(tiles, axis, split_axis=0, concat_axis=0, tiled=True)  34.3 us
    all_to_all x4, starting transfers between devices, sum_at_owner(): lax.all_to_all(in_blocks(shard, dim, devices), axis, 0, 0, tiled=True)  24.2 us
    all_to_all x4, starting transfers between devices, sent_to_all(): return lax.all_to_all(copies, axis, split_axis=0, concat_axis=0, tiled=True)  22.9 us
  transfers between devices with their start and end apart: 9, of which 8 were waited for; matrix products, arithmetic and copies ran while one was open for 1% of the time, Pallas kernels for 0%

commit v1 on v0

v1 whole, which is shorter than its diff:
```python
import functools

import jax
import jax.numpy as jnp
from jax import lax
from jax.experimental import pallas as pl
from jax.experimental.pallas import tpu as pltpu
from jax.sharding import PartitionSpec as P

ITERS = 4
PRIOR_DOF = 4.0
PRIOR_SCALE = 0.5
AXIS = "ppl"
CORES = 2
NEAR = 8
MESH = pl.DeviceIdType.MESH
F32 = jnp.float32
BF16 = jnp.bfloat16
NT = (((1,), (1,)), ((), ()))
NN = (((1,), (0,)), ((), ()))
CODES = 32000.0
FULL = (3, -3, 2, -2, 1, -1)
ENDS = (NEAR // 2, -(NEAR // 2))
SENDS = ((NEAR // 2, 3, -3), (2, -2), (1, -1), (0,))
TAKES = ((0, 1, -1), (2, -2), (3, -3, NEAR // 2))
SPLIT = True


def kernel(
    chips,
    geno,
    resid,
    npeople,
    ncoef,
    coef,
    block,
    prior,
    sigma,
    gamma,
    counts,
    coef_out,
    resid_out,
    sigma_out,
    xh,
    xo,
    cf,
    res,
    npl,
    nco,
    s_block,
    s_prior,
    s_sigma,
    s_gamma,
    s_counts,
    pres,
    dsend,
    drecv,
    rs_own,
    rs_send,
    rs_recv,
    cv_send,
    cv_recv,
    mid,
    mcv,
    ag,
    agn,
    agn_send,
    search_ref,
    dir_ref,
    dirb_ref,
    acc,
    img_send,
    img_recv,
    dd_send,
    dd_recv,
    img,
    fitted,
    fin,
    c_recv,
    d_recv,
    vals,
    load_sem,
    small_sem,
    pair_send,
    pair_recv,
    st_send,
    st_recv,
):
    traits, rows = res.shape
    width = xo.shape[2]
    half = NEAR * width
    groups = chips // NEAR
    top = traits // 2
    me = lax.axis_index(AXIS)
    z = me // CORES
    k = lax.rem(me, CORES)
    g = z // NEAR
    r = lax.rem(z, NEAR)
    partner = {AXIS: z * CORES + (1 - k)}

    def chip(offset, core):
        return {AXIS: lax.rem(z + offset + chips, chips) * CORES + core}

    def piece_at(offset):
        return lax.rem(r + offset + NEAR, NEAR)

    barrier = pltpu.get_barrier_semaphore()
    greeted = 0
    hello = (NEAR, -NEAR, *ENDS, *FULL) if SPLIT else range(1, chips)
    for offset in hello:
        pl.semaphore_signal(barrier, inc=1, device_id=chip(offset, k), device_id_type=MESH)
        greeted += 1
    for offset in (*FULL, *ENDS, 0):
        pl.semaphore_signal(barrier, inc=1, device_id=chip(offset, 1 - k), device_id_type=MESH)
        greeted += 1

    mine = pl.multiple_of(k * half, half)
    other = pl.multiple_of((1 - k) * half, half)
    own_col = pl.multiple_of(k * half + r * width, width)
    loads = [
        pltpu.make_async_copy(coef.at[:, pl.ds(mine, half)], cf.at[0], load_sem.at[0]),
        pltpu.make_async_copy(coef.at[:, pl.ds(other, half)], cf.at[1], load_sem.at[1]),
        pltpu.make_async_copy(coef.at[:, pl.ds(2 * half + mine, half)], cf.at[2], load_sem.at[2]),
        pltpu.make_async_copy(coef.at[:, pl.ds(2 * half + other, half)], cf.at[3], load_sem.at[3]),
        pltpu.make_async_copy(resid, res, load_sem.at[4]),
        pltpu.make_async_copy(npeople, npl, load_sem.at[5]),
        pltpu.make_async_copy(ncoef.at[:, pl.ds(own_col, width)], nco, load_sem.at[6]),
    ]
    for piece in range(NEAR):
        at = pl.multiple_of(mine + piece * width, width)
        loads.append(
            pltpu.make_async_copy(geno.at[:, pl.ds(at, width)], xh.at[0, piece], load_sem.at[7 + piece])
        )
    for piece in range(NEAR):
        at = pl.multiple_of(other + piece * width, width)
        loads.append(
            pltpu.make_async_copy(geno.at[:, pl.ds(at, width)], xo.at[piece], load_sem.at[15 + piece])
        )
    smalls = [
        pltpu.make_async_copy(block, s_block, small_sem.at[0]),
        pltpu.make_async_copy(prior, s_prior, small_sem.at[1]),
        pltpu.make_async_copy(sigma, s_sigma, small_sem.at[2]),
        pltpu.make_async_copy(gamma, s_gamma, small_sem.at[3]),
        pltpu.make_async_copy(counts, s_counts, small_sem.at[4]),
    ]
    for copy in smalls + loads:
        copy.start()
    for copy in smalls:
        copy.wait()

    row_id = lax.broadcasted_iota(jnp.int32, (traits, 128), 0)
    lane_id = lax.broadcasted_iota(jnp.int32, (traits, 128), 1)

    def to_row(columns):
        total = jnp.zeros((traits, 128), F32)
        for place, column in enumerate(columns):
            total += jnp.where(lane_id == row_id + place * traits, column, 0.0)
        return jnp.sum(total, axis=0, keepdims=True)

    def to_column(line, place):
        return jnp.sum(
            jnp.where(lane_id == row_id + place * traits, line, 0.0), axis=1, keepdims=True
        )

    def column_of(ref):
        column = jnp.zeros((traits, 128), F32)
        for trait in range(traits):
            column = jnp.where(row_id == trait, ref[trait], column)
        return column

    vals[0] = column_of(s_sigma)
    vals[1] = column_of(s_prior)
    vals[2] = column_of(s_gamma)
    noise_var = vals[0][:, 0:1]
    ridge = vals[1][:, 0:1]
    slot = lax.broadcasted_iota(jnp.int32, (traits, rows), 1)
    mask_own = (slot < s_counts[me]).astype(F32)
    mask_pair = (slot < s_counts[z * CORES + (1 - k)]).astype(F32)

    def coded(values):
        largest = jnp.maximum(jnp.max(jnp.abs(values), axis=1, keepdims=True), 1e-30)
        codes = jnp.round(values * (CODES / largest)).astype(jnp.int32).astype(jnp.int16)
        return codes, largest * (1.0 / CODES)

    def decoded(codes, unit):
        return codes.astype(jnp.int32).astype(F32) * unit

    for copy in loads:
        copy.wait()
    first = s_block[0] == 0
    old_mine = jnp.where(first, cf[0], cf[2]).astype(BF16)
    old_other = jnp.where(first, cf[1], cf[3]).astype(BF16)
    fitted_old = jnp.zeros((traits, rows), F32)
    for piece in range(NEAR):
        columns = slice(piece * width, (piece + 1) * width)
        fitted_old += lax.dot_general(old_mine[:, columns], xh[0, piece], NT, preferred_element_type=F32)
        fitted_old += lax.dot_general(old_other[:, columns], xo[piece], NT, preferred_element_type=F32)
    partial_res = mask_own * (res[...] + fitted_old)
    pres[0] = partial_res
    target = (mask_own * (partial_res + jnp.sqrt(noise_var) * npl[...])).astype(BF16)
    for piece in range(NEAR):
        dsend[piece] = lax.dot_general(target, xo[piece], NN, preferred_element_type=F32)
    for piece in range(NEAR):
        dir_ref[piece] = lax.dot_general(target, xh[0, piece], NN, preferred_element_type=F32)
    fitted[...] = jnp.zeros_like(fitted)
    acc[...] = jnp.zeros_like(acc)

    pl.semaphore_wait(barrier, greeted)

    def to_pair(src, dst, index):
        return pltpu.make_async_remote_copy(
            src_ref=src,
            dst_ref=dst,
            send_sem=pair_send.at[index],
            recv_sem=pair_recv.at[index],
            device_id=partner,
            device_id_type=MESH,
        )

    swap_sum = to_pair(dsend, drecv, 0)
    swap_res = to_pair(pres.at[0], pres.at[1], 1)
    swap_geno = to_pair(xo, xh.at[1], 2)
    swap_sum.start()
    swap_res.start()
    swap_geno.start()
    swap_sum.wait_recv()

    def send(src, dst, stage, number, target):
        pltpu.make_async_remote_copy(
            src_ref=src,
            dst_ref=dst,
            send_sem=st_send.at[number, stage],
            recv_sem=st_recv.at[number, stage],
            device_id=target,
            device_id_type=MESH,
        ).start()

    def arrived(ref, stage, number):
        pltpu.make_async_copy(ref, ref, st_recv.at[number, stage]).wait()

    def sum_for_owner(number, part_of, column, relay):
        for offsets in SENDS:
            pieces = [piece_at(offset) for offset in offsets]
            for offset, piece, part in zip(offsets, pieces, [part_of(piece) for piece in pieces]):
                if offset == 0:
                    rs_own[...] = part
                    continue
                rs_send[number, piece], unit = coded(part)
                cv_send[number, piece] = to_row([column, unit])
            for offset, piece in zip(offsets, pieces):
                line = cv_send.at[number, piece]
                codes = rs_send.at[number, piece]
                if offset == ENDS[0]:
                    for place, end in enumerate(ENDS):
                        band = pl.ds(place * top, top)
                        send(line, cv_recv.at[number, 6 + place], 1, number, chip(end, k))
                        send(
                            codes.at[band], rs_recv.at[number, 6, band], 0, number, chip(end, k)
                        )
                elif offset:
                    slot_id = FULL.index(offset)
                    send(line, cv_recv.at[number, slot_id], 1, number, chip(offset, k))
                    send(codes, rs_recv.at[number, slot_id], 0, number, chip(offset, k))
        arrived(cv_recv.at[number], 1, number)
        sums = to_row([column])
        for slot_id in range(7):
            sums += cv_recv[number, slot_id]
        sums = to_column(sums, 0)
        upper = lax.broadcasted_iota(jnp.int32, (traits, 1), 0) < top
        arrived(rs_recv.at[number], 0, number)
        total = rs_own[...]
        for slot_id in range(6):
            total += decoded(rs_recv[number, slot_id], to_column(cv_recv[number, slot_id], 1))
        unit = jnp.where(upper, to_column(cv_recv[number, 6], 1), to_column(cv_recv[number, 7], 1))
        total += decoded(rs_recv[number, 6], unit)
        mid[number, g], unit = coded(total)
        mcv[number, g] = to_row([sums, unit])

        def pass_on(group, offset, stage):
            send(mcv.at[number, group], mcv.at[number, group], stage + 1, number, chip(offset, k))
            send(mid.at[number, group], mid.at[number, group], stage, number, chip(offset, k))

        if not relay:
            pass_on(g, 2 * NEAR, 10)
        pass_on(g, NEAR, 2)
        pass_on(g, -NEAR, 8)
        arrived(mcv.at[number, 0], 9, number)
        arrived(mid.at[number, 0], 8, number)
        if relay:
            pass_on(lax.rem(g + 1, groups), -NEAR, 10)
        arrived(mcv.at[number, 0], 3, number)
        arrived(mid.at[number, 0], 2, number)
        arrived(mcv.at[number, 0], 11, number)
        arrived(mid.at[number, 0], 10, number)
        sums = mcv[number, 0]
        total = decoded(mid[number, 0], to_column(sums, 1))
        for group in range(1, groups):
            line = mcv[number, group]
            sums += line
            total += decoded(mid[number, group], to_column(line, 1))
        return total, to_column(sums, 0)

    def share(number, search, step):
        ag[number, r] = search.astype(BF16)
        agn_send[number] = to_row([jnp.sum(search * search, axis=1, keepdims=True), step])
        line = k * NEAR + r
        agn[number, line] = agn_send[number]
        for offset in (ENDS[0], *FULL):
            send(agn_send.at[number], agn.at[number, line], 5, number, chip(offset, k))
        for offset in (ENDS[0], *FULL, 0):
            send(agn_send.at[number], agn.at[number, line], 5, number, chip(offset, 1 - k))
        for place, end in enumerate(ENDS):
            band = pl.ds(place * top, top)
            send(ag.at[number, r, band], ag.at[number, r, band], 14, number, chip(end, k))
        for offset in FULL:
            send(ag.at[number, r], ag.at[number, r], 11 + abs(offset), number, chip(offset, k))
        arrived(agn.at[number, pl.ds(0, CORES * NEAR - 1)], 5, number)
        line = agn[number, 0]
        for place in range(1, CORES * NEAR):
            line += agn[number, place]
        return to_column(line, 0), to_column(agn[number, 0], 1)

    def image_of(number, ratio):
        squares = jnp.zeros((traits, 1), F32)
        own = jnp.zeros((traits, rows), F32)
        pair = jnp.zeros((traits, rows), F32)
        for stage, offsets in enumerate(TAKES):
            arrived(ag.at[number, pl.ds(0, len(offsets) - (0 in offsets))], 12 + stage, number)
            lows = []
            for offset in offsets:
                piece = piece_at(offset)
                direction = ag[number, piece].astype(F32)
                if ratio is not None:
                    direction += ratio * dir_ref[piece]
                low = direction.astype(BF16)
                dir_ref[piece] = direction
                dirb_ref[piece] = low
                lows.append((piece, low))
            for piece, low in lows:
                own += lax.dot_general(low, xh[0, piece], NT, preferred_element_type=F32)
                pair += lax.dot_general(low, xh[1, piece], NT, preferred_element_type=F32)
                wide = low.astype(F32)
                squares += jnp.sum(wide * wide, axis=1, keepdims=True)
        img_send[number, 0] = pair
        img_send[number, 1] = own
        dd_send[number] = to_row([squares])
        send(img_send.at[number], img_recv.at[number], 6, number, partner)
        send(dd_send.at[number], dd_recv.at[number], 7, number, partner)
        arrived(dd_recv.at[number], 7, number)
        arrived(img_recv.at[number], 6, number)
        own = mask_own * (own + img_recv[number, 0])
        pair = mask_pair * (pair + img_recv[number, 1])
        img[0] = own
        img[1] = pair
        return own, pair, to_column(dd_send[number] + dd_recv[number], 0)

    zero = jnp.zeros((traits, 1), F32)
    total, _ = sum_for_owner(0, lambda piece: dir_ref[piece] + drecv[piece], zero, SPLIT)
    search = total / noise_var + jnp.sqrt(ridge) * nco[...]
    search_ref[...] = search
    norm, _ = share(0, search, zero)
    swap_res.wait_recv()
    swap_geno.wait_recv()
    own, pair, squares = image_of(0, None)
    vals[3] = jnp.broadcast_to(norm, (traits, 128))
    vals[5] = jnp.broadcast_to(squares, (traits, 128))

    def iterate(number, carry):
        own, pair = img[0], img[1]
        squares = vals[5][:, 0:1]
        own_low = own.astype(BF16)
        pair_low = pair.astype(BF16)
        bend = jnp.sum(own * own_low.astype(F32), axis=1, keepdims=True)
        bend += jnp.sum(pair * pair_low.astype(F32), axis=1, keepdims=True)

        def part_of(piece):
            part = lax.dot_general(own_low, xh[0, piece], NN, preferred_element_type=F32)
            return part + lax.dot_general(pair_low, xh[1, piece], NN, preferred_element_type=F32)

        total, bend = sum_for_owner(number, part_of, bend, False)
        norm_now = vals[3][:, 0:1]
        step = norm_now / (bend / noise_var + ridge * squares)
        applied = total / noise_var + ridge * dirb_ref[r].astype(F32)
        search = search_ref[...] - step * applied
        search_ref[...] = search
        norm_next, step = share(number, search, step)
        acc[...] += step[None] * dirb_ref[...].astype(F32)
        fitted[...] += step[None] * img[...]
        vals[3] = jnp.broadcast_to(norm_next, (traits, 128))
        vals[4] = jnp.broadcast_to(step, (traits, 128))
        own, pair, squares = image_of(number, norm_next / norm_now)
        vals[5] = jnp.broadcast_to(squares, (traits, 128))
        return carry

    lax.fori_loop(1, ITERS, iterate, 0)

    swap_acc = to_pair(acc, c_recv, 3)
    swap_dir = to_pair(dirb_ref, d_recv, 4)
    own, pair = img[0], img[1]
    squares = vals[5][:, 0:1]
    guess = vals[4][:, 0:1]
    left_own = pres[0] - fitted[0] - guess * own
    left_pair = pres[1] - fitted[1] - guess * pair

    def both(one, two):
        return jnp.sum(one, axis=1, keepdims=True) + jnp.sum(two, axis=1, keepdims=True)

    fin[z] = to_row(
        [
            both(own * own.astype(BF16).astype(F32), pair * pair.astype(BF16).astype(F32)),
            both(left_own * left_own, left_pair * left_pair),
            both(left_own * own, left_pair * pair),
            both(own * own, pair * pair),
        ]
    )
    half_way = chips // 2
    for offset in sorted(range(1, chips), key=lambda o: -min(o, chips - o)):
        pltpu.make_async_remote_copy(
            src_ref=fin.at[z],
            dst_ref=fin.at[z],
            send_sem=pair_send.at[5],
            recv_sem=pair_recv.at[5],
            device_id=chip(offset if offset <= half_way else offset - chips, k),
            device_id_type=MESH,
        ).start()
    swap_acc.start()
    swap_dir.start()
    present = jnp.int32(0)
    for device in range(chips * CORES):
        present += s_counts[device]
    others = fin.at[pl.ds(0, chips - 1)]
    pltpu.make_async_copy(others, others, pair_recv.at[5]).wait()
    line = fin[0]
    for place in range(1, chips):
        line += fin[place]
    norm_now = vals[3][:, 0:1]
    step = norm_now / (to_column(line, 0) / noise_var + ridge * squares)
    shift = step - guess
    left = to_column(line, 1) - 2.0 * shift * to_column(line, 2) + shift * shift * to_column(line, 3)
    scale = (present.astype(F32) + PRIOR_DOF) * vals[2][:, 0:1]
    sigma_out[...] = to_row([(left + PRIOR_DOF * PRIOR_SCALE) / scale])
    resid_out[...] = pres[0] - (fitted[0] + step * own)
    for piece in range(NEAR):
        at = pl.multiple_of(mine + piece * width, width)
        coef_out[:, pl.ds(at, width)] = acc[piece] + step * dirb_ref[piece].astype(F32)
    swap_acc.wait_recv()
    swap_dir.wait_recv()
    for piece in range(NEAR):
        at = pl.multiple_of(other + piece * width, width)
        coef_out[:, pl.ds(at, width)] = c_recv[piece] + step * d_recv[piece].astype(F32)

    for swap in (swap_sum, swap_res, swap_geno, swap_acc, swap_dir):
        swap.wait_send()
    pltpu.make_async_copy(others, others, pair_send.at[5]).wait()

    def sent(ref, stage, number):
        pltpu.make_async_copy(ref, ref, st_send.at[number, stage]).wait()

    def drain(number, carry):
        sent(rs_recv.at[number], 0, number)
        sent(cv_recv.at[number], 1, number)
        for stage in (2, 8, 10):
            sent(mid.at[number, 0], stage, number)
            sent(mcv.at[number, 0], stage + 1, number)
        sent(agn.at[number, pl.ds(0, CORES * NEAR - 1)], 5, number)
        sent(img_recv.at[number], 6, number)
        sent(dd_recv.at[number], 7, number)
        for stage, offsets in enumerate(TAKES):
            sent(ag.at[number, pl.ds(0, len(offsets) - (0 in offsets))], 12 + stage, number)
        return carry

    lax.fori_loop(0, ITERS, drain, 0)


def update(geno, resid, npeople, ncoef, coef, block, prior, sigma, gamma, counts):
    rows, batch = geno.shape
    traits = resid.shape[0]
    devices = lax.axis_size(AXIS)
    chips = devices // CORES
    half = batch // CORES
    width = half // NEAR
    groups = chips // NEAR
    outside = pl.BlockSpec(memory_space=pltpu.HBM)
    inside = pl.BlockSpec(memory_space=pltpu.VMEM)
    block16 = (NEAR, traits, width)
    return pl.pallas_call(
        functools.partial(kernel, chips),
        name="gibbs",
        out_shape=(
            jax.ShapeDtypeStruct((traits, batch), F32),
            jax.ShapeDtypeStruct((traits, rows), F32),
            jax.ShapeDtypeStruct((1, 128), F32),
        ),
        in_specs=[outside] * 10,
        out_specs=(inside,) * 3,
        scratch_shapes=[
            pltpu.VMEM((2, NEAR, rows, width), BF16),
            pltpu.VMEM((NEAR, rows, width), BF16),
            pltpu.VMEM((4, traits, half), F32),
            pltpu.VMEM((traits, rows), F32),
            pltpu.VMEM((traits, rows), F32),
            pltpu.VMEM((traits, width), F32),
            pltpu.SMEM((1,), jnp.int32),
            pltpu.SMEM((traits,), F32),
            pltpu.SMEM((traits,), F32),
            pltpu.SMEM((traits,), F32),
            pltpu.SMEM((devices,), jnp.int32),
            pltpu.VMEM((2, traits, rows), F32),
            pltpu.VMEM(block16, F32),
            pltpu.VMEM(block16, F32),
            pltpu.VMEM((traits, width), F32),
            pltpu.VMEM((ITERS, *block16), jnp.int16),
            pltpu.VMEM((ITERS, 7, traits, width), jnp.int16),
            pltpu.VMEM((ITERS, NEAR, 1, 128), F32),
            pltpu.VMEM((ITERS, 8, 1, 128), F32),
            pltpu.VMEM((ITERS, groups, traits, width), jnp.int16),
            pltpu.VMEM((ITERS, groups, 1, 128), F32),
            pltpu.VMEM((ITERS, *block16), BF16),
            pltpu.VMEM((ITERS, CORES * NEAR, 1, 128), F32),
            pltpu.VMEM((ITERS, 1, 128), F32),
            pltpu.VMEM((traits, width), F32),
            pltpu.VMEM(block16, F32),
            pltpu.VMEM(block16, BF16),
            pltpu.VMEM(block16, F32),
            pltpu.VMEM((ITERS, 2, traits, rows), F32),
            pltpu.VMEM((ITERS, 2, traits, rows), F32),
            pltpu.VMEM((ITERS, 1, 128), F32),
            pltpu.VMEM((ITERS, 1, 128), F32),
            pltpu.VMEM((2, traits, rows), F32),
            pltpu.VMEM((2, traits, rows), F32),
            pltpu.VMEM((chips, 1, 128), F32),
            pltpu.VMEM(block16, F32),
            pltpu.VMEM(block16, BF16),
            pltpu.VMEM((6, traits, 128), F32),
            pltpu.SemaphoreType.DMA((23,)),
            pltpu.SemaphoreType.DMA((5,)),
            pltpu.SemaphoreType.DMA((6,)),
            pltpu.SemaphoreType.DMA((6,)),
            pltpu.SemaphoreType.DMA((ITERS, 15)),
            pltpu.SemaphoreType.DMA((ITERS, 15)),
        ],
        compiler_params=pltpu.CompilerParams(
            collective_id=0, has_side_effects=True, vmem_limit_bytes=67043328
        ),
    )(geno, resid, npeople, ncoef, coef, block, prior, sigma, gamma, counts)


def per_device(geno, resid, npeople, ncoef, coef, block, prior, sigma, gamma, counts):
    batch = geno.shape[1]
    batch_coef, resid_new, sigma_line = update(
        geno, resid, npeople, ncoef, coef, block, prior, sigma, gamma, counts
    )
    coef_new = lax.dynamic_update_slice_in_dim(coef, batch_coef, block[0] * batch, 1)
    return coef_new, resid_new, sigma_line[0, : resid.shape[0]]


def solution(mesh):
    return jax.shard_map(
        per_device,
        mesh=mesh,
        in_specs=(
            P(("trait", "ppl"), None),
            P("trait", "ppl"),
            P("trait", "ppl"),
            P("trait", None),
            P("trait", None),
            P("trait"),
            P("trait"),
            P("trait"),
            P("trait"),
            P("trait"),
        ),
        out_specs=(P("trait", None), P("trait", "ppl"), P("trait")),
        check_vma=False,
    )
```

time: 830 us -> 159 us (0.19)
  blocking collectives: 389 us -> 0 us
  waiting for transfers between devices: 300 us -> 0 us
  Pallas kernels: 0 us -> 148 us
  starting transfers between devices: 81.4 us -> 0 us
  local copies, waits for them, and re-layouts: 30.5 us -> 6.66 us
  other arithmetic: 9.41 us -> 0 us
    all_to_all x9 -> x0, blocking collectives: 328 us -> none  [sent_to_all(): return lax.all_to_all(copies, axis, split_axis=0, concat_axis=0, tiled=True)]
    all_to_all x9 -> x0, waiting for transfers between devices: 300 us -> none  [the longest x4 171 us: sum_at_owner(): lax.all_to_all(in_blocks(shard, dim, devices), axis, 0, 0, tiled=True)]
    pallas_call x0 -> x1, Pallas kernels: none -> 148 us  [update(): pl.pallas_call(functools.partial(kernel, chips), name='gibbs', out_shape=...]
    all_to_all x9 -> x0, starting transfers between devices: 81.4 us -> none  [the longest x1 34.3 us: sent_and_summed(): lax.all_to_all(tiles, axis, split_axis=0, concat_axis=0, tiled=True)]
    all_gather x1 -> x0, blocking collectives: 60.8 us -> none  [per_device(): batch_coef = lax.all_gather(coef_share, 'ppl', axis=1, tiled=True)]
    unnamed x36 -> x2, local copies, waits for them, and re-layouts: 14.6 us -> 3.64 us
    reshape x14 -> x0, local copies, waits for them, and re-layouts: 8.43 us -> none  [the longest x10 6.6 us: in_blocks(): shard.reshape(*lengths[:dim], devices, lengths[dim] // devices, *lengths[...]
  transfers between devices with their start and end apart: 9 -> 0, of which waited for: 8 -> 0; matrix products, arithmetic and copies ran while one was open for 1% -> 0% of each run, Pallas kernels for 0% -> 0%
where the time goes in v1:
time: 159 us; the launch traced here: 156 us
  Pallas kernels  148 us (93%)
  local copies, waits for them, and re-layouts  6.66 us (4%)
    pallas_call x1, Pallas kernels, update(): pl.pallas_call(functools.partial(kernel, chips), name='gibbs', out_shape=...  148 us
    unnamed x2, local copies, waits for them, and re-layouts  3.64 us

profile of v1, /device:TPU:37, one launch (start us, length us, event | category | flops | bytes accessed | tf_op | source)
XLA Modules:
  0.0 156.4 jit_solution(1878547293520056687)
XLA Ops:
  0.6 2.3 %copy.17.coef = f32[32,8192]{1,0:T(8,128)} copy(f32[32,8192]{1,0:T(8,128)} %param.14) | data formatting | bytes 2097152
  3.5 148.5 %gibbs.1 = (f32[32,4096]{1,0:T(8,128)}, f32[32,256]{1,0:T(8,128)}, f32[1,128]{1,0:T(1,128)}) custom-call(bf16[256,4096]{1,0:T(8,128)(2,1)} %geno.1, f32[32,256]{1,0:T(8,128)} %resid.1, f32[32,256]{1,0:T(8,128)} %npeople.1, f32[32,4096]{1,0:T(8,128)} %ncoef.1, f32[32,8192]{1,0:T(8,128)} %copy.17.coef, s32[1]{0:T(128)S(6)} %copy.16.block, f32[32]{0:T(128)} %prior.1, ...), custom_call_target="tpu_custom_call" | custom-call | tf_op jit(solution)/shard_map/gibbs/pallas_call | solution.py:486
  152.0 1.9 %constant_dynamic-update-slice_fusion = f32[32,8192]{1,0:T(8,128)} fusion(f32[32,8192]{1,0:T(8,128)} %copy.17.coef, f32[32,4096]{1,0:T(8,128)} %get-tuple-element.6, s32[]{:T(128)S(6)} %select_n.3), kind=kLoop, calls=%fused_computation.1 | loop fusion | bytes 1048580 | tf_op jit(solution)/shard_map/dynamic_update_slice | solution.py:553
  153.9 1.1 slice_bitcast_fusion
  155.0 1.4 copy.18

commit v2 on v1

--- a/solution.py
+++ b/solution.py
@@ -23,7 +23,7 @@
 ENDS = (NEAR // 2, -(NEAR // 2))
 SENDS = ((NEAR // 2, 3, -3), (2, -2), (1, -1), (0,))
 TAKES = ((0, 1, -1), (2, -2), (3, -3, NEAR // 2))
-SPLIT = True
+TAKE_OF = {sign * abs(o): 12 + i for i, offsets in enumerate(TAKES) for o in offsets for sign in (1, -1)}
 
 
 def kernel(
@@ -64,7 +64,8 @@
     mcv,
     ag,
     agn,
-    agn_send,
+    pn_send,
+    pn_recv,
     search_ref,
     dir_ref,
     dirb_ref,
@@ -96,27 +97,23 @@
     k = lax.rem(me, CORES)
     g = z // NEAR
     r = lax.rem(z, NEAR)
+    role = lax.rem(k + z // (NEAR // 2), CORES)
     partner = {AXIS: z * CORES + (1 - k)}
 
-    def chip(offset, core):
-        return {AXIS: lax.rem(z + offset + chips, chips) * CORES + core}
+    def chip(offset):
+        there = lax.rem(z + offset + chips, chips)
+        return {AXIS: there * CORES + lax.rem(role + there // (NEAR // 2), CORES)}
 
     def piece_at(offset):
         return lax.rem(r + offset + NEAR, NEAR)
 
     barrier = pltpu.get_barrier_semaphore()
-    greeted = 0
-    hello = (NEAR, -NEAR, *ENDS, *FULL) if SPLIT else range(1, chips)
-    for offset in hello:
-        pl.semaphore_signal(barrier, inc=1, device_id=chip(offset, k), device_id_type=MESH)
-        greeted += 1
-    for offset in (*FULL, *ENDS, 0):
-        pl.semaphore_signal(barrier, inc=1, device_id=chip(offset, 1 - k), device_id_type=MESH)
-        greeted += 1
-
-    mine = pl.multiple_of(k * half, half)
-    other = pl.multiple_of((1 - k) * half, half)
-    own_col = pl.multiple_of(k * half + r * width, width)
+    for target in (*[chip(offset) for offset in (*ENDS, *FULL)], partner):
+        pl.semaphore_signal(barrier, inc=1, device_id=target, device_id_type=MESH)
+
+    mine = pl.multiple_of(role * half, half)
+    other = pl.multiple_of((1 - role) * half, half)
+    own_col = pl.multiple_of(role * half + r * width, width)
     loads = [
         pltpu.make_async_copy(coef.at[:, pl.ds(mine, half)], cf.at[0], load_sem.at[0]),
         pltpu.make_async_copy(coef.at[:, pl.ds(other, half)], cf.at[1], load_sem.at[1]),
@@ -205,7 +202,7 @@
     fitted[...] = jnp.zeros_like(fitted)
     acc[...] = jnp.zeros_like(acc)
 
-    pl.semaphore_wait(barrier, greeted)
+    pl.semaphore_wait(barrier, len(ENDS) + len(FULL) + 1)
 
     def to_pair(src, dst, index):
         return pltpu.make_async_remote_copy(
@@ -253,14 +250,14 @@
                 if offset == ENDS[0]:
                     for place, end in enumerate(ENDS):
                         band = pl.ds(place * top, top)
-                        send(line, cv_recv.at[number, 6 + place], 1, number, chip(end, k))
+                        send(line, cv_recv.at[number, 6 + place], 1, number, chip(end))
                         send(
-                            codes.at[band], rs_recv.at[number, 6, band], 0, number, chip(end, k)
+                            codes.at[band], rs_recv.at[number, 6, band], 0, number, chip(end)
                         )
                 elif offset:
                     slot_id = FULL.index(offset)
-                    send(line, cv_recv.at[number, slot_id], 1, number, chip(offset, k))
-                    send(codes, rs_recv.at[number, slot_id], 0, number, chip(offset, k))
+                    send(line, cv_recv.at[number, slot_id], 1, number, chip(offset))
+                    send(codes, rs_recv.at[number, slot_id], 0, number, chip(offset))
         arrived(cv_recv.at[number], 1, number)
         sums = to_row([column])
         for slot_id in range(7):
@@ -277,8 +274,8 @@
         mcv[number, g] = to_row([sums, unit])
 
         def pass_on(group, offset, stage):
-            send(mcv.at[number, group], mcv.at[number, group], stage + 1, number, chip(offset, k))
-            send(mid.at[number, group], mid.at[number, group], stage, number, chip(offset, k))
+            send(mcv.at[number, group], mcv.at[number, group], stage + 1, number, chip(offset))
+            send(mid.at[number, group], mid.at[number, group], stage, number, chip(offset))
 
         if not relay:
             pass_on(g, 2 * NEAR, 10)
@@ -302,21 +299,22 @@
 
     def share(number, search, step):
         ag[number, r] = search.astype(BF16)
-        agn_send[number] = to_row([jnp.sum(search * search, axis=1, keepdims=True), step])
-        line = k * NEAR + r
-        agn[number, line] = agn_send[number]
-        for offset in (ENDS[0], *FULL):
-            send(agn_send.at[number], agn.at[number, line], 5, number, chip(offset, k))
-        for offset in (ENDS[0], *FULL, 0):
-            send(agn_send.at[number], agn.at[number, line], 5, number, chip(offset, 1 - k))
         for place, end in enumerate(ENDS):
             band = pl.ds(place * top, top)
-            send(ag.at[number, r, band], ag.at[number, r, band], 14, number, chip(end, k))
+            send(ag.at[number, r, band], ag.at[number, r, band], TAKE_OF[end], number, chip(end))
         for offset in FULL:
-            send(ag.at[number, r], ag.at[number, r], 11 + abs(offset), number, chip(offset, k))
-        arrived(agn.at[number, pl.ds(0, CORES * NEAR - 1)], 5, number)
+            send(ag.at[number, r], ag.at[number, r], TAKE_OF[offset], number, chip(offset))
+        pn_send[number] = to_row([jnp.sum(search * search, axis=1, keepdims=True), step])
+        send(pn_send.at[number], pn_recv.at[number], 15, number, partner)
+        arrived(pn_recv.at[number], 15, number)
+        here, there = pn_send[number], pn_recv[number]
+        steps = jnp.where(role == 0, here, there)
+        agn[number, r] = jnp.where(lane_id[0:1] < traits, here + there, steps)
+        for offset in (ENDS[0], *FULL):
+            send(agn.at[number, r], agn.at[number, r], 5, number, chip(offset))
+        arrived(agn.at[number, pl.ds(0, NEAR - 1)], 5, number)
         line = agn[number, 0]
-        for place in range(1, CORES * NEAR):
+        for place in range(1, NEAR):
             line += agn[number, place]
         return to_column(line, 0), to_column(agn[number, 0], 1)
 
@@ -355,7 +353,7 @@
         return own, pair, to_column(dd_send[number] + dd_recv[number], 0)
 
     zero = jnp.zeros((traits, 1), F32)
-    total, _ = sum_for_owner(0, lambda piece: dir_ref[piece] + drecv[piece], zero, SPLIT)
+    total, _ = sum_for_owner(0, lambda piece: dir_ref[piece] + drecv[piece], zero, True)
     search = total / noise_var + jnp.sqrt(ridge) * nco[...]
     search_ref[...] = search
     norm, _ = share(0, search, zero)
@@ -420,7 +418,7 @@
             dst_ref=fin.at[z],
             send_sem=pair_send.at[5],
             recv_sem=pair_recv.at[5],
-            device_id=chip(offset if offset <= half_way else offset - chips, k),
+            device_id=chip(offset if offset <= half_way else offset - chips),
             device_id_type=MESH,
         ).start()
     swap_acc.start()
@@ -440,14 +438,20 @@
     scale = (present.astype(F32) + PRIOR_DOF) * vals[2][:, 0:1]
     sigma_out[...] = to_row([(left + PRIOR_DOF * PRIOR_SCALE) / scale])
     resid_out[...] = pres[0] - (fitted[0] + step * own)
-    for piece in range(NEAR):
-        at = pl.multiple_of(mine + piece * width, width)
-        coef_out[:, pl.ds(at, width)] = acc[piece] + step * dirb_ref[piece].astype(F32)
+
+    def put(start, place, steps, directions):
+        for piece in range(NEAR):
+            columns = slice(piece * width, (piece + 1) * width)
+            new = steps[piece] + step * directions[piece].astype(F32)
+            at = pl.multiple_of(start + piece * width, width)
+            coef_out[:, pl.ds(at, width)] = jnp.where(first, new, cf[place, :, columns])
+            at = pl.multiple_of(CORES * half + start + piece * width, width)
+            coef_out[:, pl.ds(at, width)] = jnp.where(first, cf[place + 2, :, columns], new)
+
+    put(mine, 0, acc, dirb_ref)
     swap_acc.wait_recv()
     swap_dir.wait_recv()
-    for piece in range(NEAR):
-        at = pl.multiple_of(other + piece * width, width)
-        coef_out[:, pl.ds(at, width)] = c_recv[piece] + step * d_recv[piece].astype(F32)
+    put(other, 1, c_recv, d_recv)
 
     for swap in (swap_sum, swap_res, swap_geno, swap_acc, swap_dir):
         swap.wait_send()
@@ -462,7 +466,8 @@
         for stage in (2, 8, 10):
             sent(mid.at[number, 0], stage, number)
             sent(mcv.at[number, 0], stage + 1, number)
-        sent(agn.at[number, pl.ds(0, CORES * NEAR - 1)], 5, number)
+        sent(agn.at[number, pl.ds(0, NEAR - 1)], 5, number)
+        sent(pn_recv.at[number], 15, number)
         sent(img_recv.at[number], 6, number)
         sent(dd_recv.at[number], 7, number)
         for stage, offsets in enumerate(TAKES):
@@ -487,7 +492,7 @@
         functools.partial(kernel, chips),
         name="gibbs",
         out_shape=(
-            jax.ShapeDtypeStruct((traits, batch), F32),
+            jax.ShapeDtypeStruct(coef.shape, F32),
             jax.ShapeDtypeStruct((traits, rows), F32),
             jax.ShapeDtypeStruct((1, 128), F32),
         ),
@@ -516,7 +521,8 @@
             pltpu.VMEM((ITERS, groups, traits, width), jnp.int16),
             pltpu.VMEM((ITERS, groups, 1, 128), F32),
             pltpu.VMEM((ITERS, *block16), BF16),
-            pltpu.VMEM((ITERS, CORES * NEAR, 1, 128), F32),
+            pltpu.VMEM((ITERS, NEAR, 1, 128), F32),
+            pltpu.VMEM((ITERS, 1, 128), F32),
             pltpu.VMEM((ITERS, 1, 128), F32),
             pltpu.VMEM((traits, width), F32),
             pltpu.VMEM(block16, F32),
@@ -536,21 +542,19 @@
             pltpu.SemaphoreType.DMA((5,)),
             pltpu.SemaphoreType.DMA((6,)),
             pltpu.SemaphoreType.DMA((6,)),
-            pltpu.SemaphoreType.DMA((ITERS, 15)),
-            pltpu.SemaphoreType.DMA((ITERS, 15)),
+            pltpu.SemaphoreType.DMA((ITERS, 16)),
+            pltpu.SemaphoreType.DMA((ITERS, 16)),
         ],
         compiler_params=pltpu.CompilerParams(
-            collective_id=0, has_side_effects=True, vmem_limit_bytes=67043328
+            collective_id=0, has_side_effects=True, vmem_limit_bytes=64 * 1024 * 1000
         ),
     )(geno, resid, npeople, ncoef, coef, block, prior, sigma, gamma, counts)
 
 
 def per_device(geno, resid, npeople, ncoef, coef, block, prior, sigma, gamma, counts):
-    batch = geno.shape[1]
-    batch_coef, resid_new, sigma_line = update(
+    coef_new, resid_new, sigma_line = update(
         geno, resid, npeople, ncoef, coef, block, prior, sigma, gamma, counts
     )
-    coef_new = lax.dynamic_update_slice_in_dim(coef, batch_coef, block[0] * batch, 1)
     return coef_new, resid_new, sigma_line[0, : resid.shape[0]]
 
 

time: 159 us -> 161 us (1.013); the launches traced: 156 us -> 161 us
  Pallas kernels: 148 us -> 156 us
  local copies, waits for them, and re-layouts: 6.66 us -> 3.97 us
    pallas_call x1, Pallas kernels: 148 us -> 156 us  [update(): pl.pallas_call(functools.partial(kernel, chips), name='gibbs', out_shape=...]
    dynamic_update_slice x1 -> x0, local copies, waits for them, and re-layouts: 1.88 us -> none  [per_device(): lax.dynamic_update_slice_in_dim(coef, batch_coef, block[0] * batch, 1)]
    unnamed x2 -> x4, local copies, waits for them, and re-layouts: 3.64 us -> 2.88 us
where the time goes in v2:
time: 161 us
  Pallas kernels  156 us (97%)
  local copies, waits for them, and re-layouts  3.97 us (2%)
    pallas_call x1, Pallas kernels, update(): pl.pallas_call(functools.partial(kernel, chips), name='gibbs', out_shape=...  156 us

profile of v2, /device:TPU:37, one launch (start us, length us, event | category | flops | bytes accessed | tf_op | source)
XLA Modules:
  0.0 161.2 jit_solution(3826074588786783050)
XLA Ops:
  1.3 156.0 %gibbs.1 = (f32[32,8192]{1,0:T(8,128)}, f32[32,256]{1,0:T(8,128)}, f32[1,128]{1,0:T(1,128)}) custom-call(bf16[256,4096]{1,0:T(8,128)(2,1)} %geno.1, f32[32,256]{1,0:T(8,128)} %resid.1, f32[32,256]{1,0:T(8,128)} %npeople.1, f32[32,4096]{1,0:T(8,128)} %ncoef.1, f32[32,8192]{1,0:T(8,128)} %coef.1, s32[1]{0:T(128)S(6)} %copy.15.block, f32[32]{0:T(128)} %prior.1, ...), custom_call_target="tpu_custom_call" | custom-call | tf_op jit(solution)/shard_map/gibbs/pallas_call | solution.py:491
  157.3 0.0 copy-start
  157.3 1.1 slice_bitcast_fusion
  158.4 2.3 %copy.16 = f32[32,8192]{1,0:T(8,128)} copy(f32[32,8192]{1,0:T(8,128)} %get-tuple-element.12) | data formatting | bytes 2097152
  160.6 0.0 copy-done
  160.6 0.6 copy.17
Async XLA Ops:
  157.3 3.4 %copy-start = (f32[32,256]{1,0:T(8,128)S(1)}, f32[32,256]{1,0:T(8,128)}, u32[]{:S(2)}) copy-start(f32[32,256]{1,0:T(8,128)} %get-tuple-element.13) | copy-start | bytes 98308

commit v3 on v2

--- a/solution.py
+++ b/solution.py
@@ -64,11 +64,8 @@
     mcv,
     ag,
     agn,
-    pn_send,
-    pn_recv,
     search_ref,
     dir_ref,
-    dirb_ref,
     acc,
     img_send,
     img_recv,
@@ -97,12 +94,10 @@
     k = lax.rem(me, CORES)
     g = z // NEAR
     r = lax.rem(z, NEAR)
-    role = lax.rem(k + z // (NEAR // 2), CORES)
     partner = {AXIS: z * CORES + (1 - k)}
 
     def chip(offset):
-        there = lax.rem(z + offset + chips, chips)
-        return {AXIS: there * CORES + lax.rem(role + there // (NEAR // 2), CORES)}
+        return {AXIS: lax.rem(z + offset + chips, chips) * CORES + k}
 
     def piece_at(offset):
         return lax.rem(r + offset + NEAR, NEAR)
@@ -111,9 +106,9 @@
     for target in (*[chip(offset) for offset in (*ENDS, *FULL)], partner):
         pl.semaphore_signal(barrier, inc=1, device_id=target, device_id_type=MESH)
 
-    mine = pl.multiple_of(role * half, half)
-    other = pl.multiple_of((1 - role) * half, half)
-    own_col = pl.multiple_of(role * half + r * width, width)
+    mine = pl.multiple_of(k * half, half)
+    other = pl.multiple_of((1 - k) * half, half)
+    own_col = pl.multiple_of(k * half + r * width, width)
     loads = [
         pltpu.make_async_copy(coef.at[:, pl.ds(mine, half)], cf.at[0], load_sem.at[0]),
         pltpu.make_async_copy(coef.at[:, pl.ds(other, half)], cf.at[1], load_sem.at[1]),
@@ -235,7 +230,7 @@
     def arrived(ref, stage, number):
         pltpu.make_async_copy(ref, ref, st_recv.at[number, stage]).wait()
 
-    def sum_for_owner(number, part_of, column, relay):
+    def sum_for_owner(number, part_of, column, relay, meanwhile=lambda: None):
         for offsets in SENDS:
             pieces = [piece_at(offset) for offset in offsets]
             for offset, piece, part in zip(offsets, pieces, [part_of(piece) for piece in pieces]):
@@ -258,6 +253,7 @@
                     slot_id = FULL.index(offset)
                     send(line, cv_recv.at[number, slot_id], 1, number, chip(offset))
                     send(codes, rs_recv.at[number, slot_id], 0, number, chip(offset))
+        meanwhile()
         arrived(cv_recv.at[number], 1, number)
         sums = to_row([column])
         for slot_id in range(7):
@@ -299,73 +295,81 @@
 
     def share(number, search, step):
         ag[number, r] = search.astype(BF16)
+        agn[number, r] = to_row([jnp.sum(search * search, axis=1, keepdims=True), step])
         for place, end in enumerate(ENDS):
             band = pl.ds(place * top, top)
             send(ag.at[number, r, band], ag.at[number, r, band], TAKE_OF[end], number, chip(end))
+            if place == 0:
+                send(agn.at[number, r], agn.at[number, r], 5, number, chip(end))
         for offset in FULL:
             send(ag.at[number, r], ag.at[number, r], TAKE_OF[offset], number, chip(offset))
-        pn_send[number] = to_row([jnp.sum(search * search, axis=1, keepdims=True), step])
-        send(pn_send.at[number], pn_recv.at[number], 15, number, partner)
-        arrived(pn_recv.at[number], 15, number)
-        here, there = pn_send[number], pn_recv[number]
-        steps = jnp.where(role == 0, here, there)
-        agn[number, r] = jnp.where(lane_id[0:1] < traits, here + there, steps)
-        for offset in (ENDS[0], *FULL):
             send(agn.at[number, r], agn.at[number, r], 5, number, chip(offset))
+
+    def image_of(number, fresh):
+        own = jnp.zeros((traits, rows), F32)
+        pair = jnp.zeros((traits, rows), F32)
+        squares = jnp.zeros((traits, 1), F32)
+        cross = jnp.zeros((traits, 1), F32)
+        for stage, offsets in enumerate(TAKES):
+            arrived(ag.at[number, pl.ds(0, len(offsets) - (0 in offsets))], 12 + stage, number)
+            for offset in offsets:
+                piece = piece_at(offset)
+                low = ag[number, piece]
+                own += lax.dot_general(low, xh[0, piece], NT, preferred_element_type=F32)
+                pair += lax.dot_general(low, xh[1, piece], NT, preferred_element_type=F32)
+                wide = low.astype(F32)
+                squares += jnp.sum(wide * wide, axis=1, keepdims=True)
+                if not fresh:
+                    cross += jnp.sum(wide * dir_ref[piece], axis=1, keepdims=True)
+        img_send[number, 0] = pair
+        img_send[number, 1] = own
+        send(img_send.at[number], img_recv.at[number], 6, number, partner)
         arrived(agn.at[number, pl.ds(0, NEAR - 1)], 5, number)
         line = agn[number, 0]
         for place in range(1, NEAR):
             line += agn[number, place]
-        return to_column(line, 0), to_column(agn[number, 0], 1)
-
-    def image_of(number, ratio):
-        squares = jnp.zeros((traits, 1), F32)
-        own = jnp.zeros((traits, rows), F32)
-        pair = jnp.zeros((traits, rows), F32)
-        for stage, offsets in enumerate(TAKES):
-            arrived(ag.at[number, pl.ds(0, len(offsets) - (0 in offsets))], 12 + stage, number)
-            lows = []
-            for offset in offsets:
-                piece = piece_at(offset)
-                direction = ag[number, piece].astype(F32)
-                if ratio is not None:
-                    direction += ratio * dir_ref[piece]
-                low = direction.astype(BF16)
-                dir_ref[piece] = direction
-                dirb_ref[piece] = low
-                lows.append((piece, low))
-            for piece, low in lows:
-                own += lax.dot_general(low, xh[0, piece], NT, preferred_element_type=F32)
-                pair += lax.dot_general(low, xh[1, piece], NT, preferred_element_type=F32)
-                wide = low.astype(F32)
-                squares += jnp.sum(wide * wide, axis=1, keepdims=True)
-        img_send[number, 0] = pair
-        img_send[number, 1] = own
-        dd_send[number] = to_row([squares])
-        send(img_send.at[number], img_recv.at[number], 6, number, partner)
+        dd_send[number] = to_row([to_column(line, 0), squares, cross])
         send(dd_send.at[number], dd_recv.at[number], 7, number, partner)
+        step = to_column(agn[number, 0], 1)
+        if not fresh:
+            fitted[...] += step[None] * img[...]
+            acc[...] += step[None] * dir_ref[...]
         arrived(dd_recv.at[number], 7, number)
+        line = dd_send[number] + dd_recv[number]
+        norm = to_column(line, 0)
+        squares = to_column(line, 1)
         arrived(img_recv.at[number], 6, number)
         own = mask_own * (own + img_recv[number, 0])
         pair = mask_pair * (pair + img_recv[number, 1])
+        if fresh:
+            ratio = jnp.zeros((traits, 1), F32)
+        else:
+            ratio = norm / vals[3][:, 0:1]
+            own += ratio * img[0]
+            pair += ratio * img[1]
+            squares += ratio * (2.0 * to_column(line, 2) + ratio * vals[5][:, 0:1])
         img[0] = own
         img[1] = pair
-        return own, pair, to_column(dd_send[number] + dd_recv[number], 0)
+        vals[3] = jnp.broadcast_to(norm, (traits, 128))
+        vals[4] = jnp.broadcast_to(step, (traits, 128))
+        vals[5] = jnp.broadcast_to(squares, (traits, 128))
+        vals[6] = jnp.broadcast_to(ratio, (traits, 128))
+
+    def turn(number):
+        dir_ref[...] = ag[number].astype(F32) + vals[6][:, 0:1][None] * dir_ref[...]
 
     zero = jnp.zeros((traits, 1), F32)
     total, _ = sum_for_owner(0, lambda piece: dir_ref[piece] + drecv[piece], zero, True)
     search = total / noise_var + jnp.sqrt(ridge) * nco[...]
     search_ref[...] = search
-    norm, _ = share(0, search, zero)
+    share(0, search, zero)
     swap_res.wait_recv()
     swap_geno.wait_recv()
-    own, pair, squares = image_of(0, None)
-    vals[3] = jnp.broadcast_to(norm, (traits, 128))
-    vals[5] = jnp.broadcast_to(squares, (traits, 128))
+    image_of(0, True)
+    dir_ref[...] = jnp.zeros_like(dir_ref)
 
     def iterate(number, carry):
         own, pair = img[0], img[1]
-        squares = vals[5][:, 0:1]
         own_low = own.astype(BF16)
         pair_low = pair.astype(BF16)
         bend = jnp.sum(own * own_low.astype(F32), axis=1, keepdims=True)
@@ -375,25 +379,23 @@
             part = lax.dot_general(own_low, xh[0, piece], NN, preferred_element_type=F32)
             return part + lax.dot_general(pair_low, xh[1, piece], NN, preferred_element_type=F32)
 
-        total, bend = sum_for_owner(number, part_of, bend, False)
-        norm_now = vals[3][:, 0:1]
-        step = norm_now / (bend / noise_var + ridge * squares)
-        applied = total / noise_var + ridge * dirb_ref[r].astype(F32)
+        def meanwhile():
+            turn(number - 1)
+
+        total, bend = sum_for_owner(number, part_of, bend, False, meanwhile)
+        step = vals[3][:, 0:1] / (bend / noise_var + ridge * vals[5][:, 0:1])
+        applied = total / noise_var + ridge * dir_ref[r]
         search = search_ref[...] - step * applied
         search_ref[...] = search
-        norm_next, step = share(number, search, step)
-        acc[...] += step[None] * dirb_ref[...].astype(F32)
-        fitted[...] += step[None] * img[...]
-        vals[3] = jnp.broadcast_to(norm_next, (traits, 128))
-        vals[4] = jnp.broadcast_to(step, (traits, 128))
-        own, pair, squares = image_of(number, norm_next / norm_now)
-        vals[5] = jnp.broadcast_to(squares, (traits, 128))
+        share(number, search, step)
+        image_of(number, False)
         return carry
 
     lax.fori_loop(1, ITERS, iterate, 0)
+    turn(ITERS - 1)
 
     swap_acc = to_pair(acc, c_recv, 3)
-    swap_dir = to_pair(dirb_ref, d_recv, 4)
+    swap_dir = to_pair(dir_ref, d_recv, 4)
     own, pair = img[0], img[1]
     squares = vals[5][:, 0:1]
     guess = vals[4][:, 0:1]
@@ -442,13 +444,13 @@
     def put(start, place, steps, directions):
         for piece in range(NEAR):
             columns = slice(piece * width, (piece + 1) * width)
-            new = steps[piece] + step * directions[piece].astype(F32)
+            new = steps[piece] + step * directions[piece]
             at = pl.multiple_of(start + piece * width, width)
             coef_out[:, pl.ds(at, width)] = jnp.where(first, new, cf[place, :, columns])
             at = pl.multiple_of(CORES * half + start + piece * width, width)
             coef_out[:, pl.ds(at, width)] = jnp.where(first, cf[place + 2, :, columns], new)
 
-    put(mine, 0, acc, dirb_ref)
+    put(mine, 0, acc, dir_ref)
     swap_acc.wait_recv()
     swap_dir.wait_recv()
     put(other, 1, c_recv, d_recv)
@@ -467,7 +469,6 @@
             sent(mid.at[number, 0], stage, number)
             sent(mcv.at[number, 0], stage + 1, number)
         sent(agn.at[number, pl.ds(0, NEAR - 1)], 5, number)
-        sent(pn_recv.at[number], 15, number)
         sent(img_recv.at[number], 6, number)
         sent(dd_recv.at[number], 7, number)
         for stage, offsets in enumerate(TAKES):
@@ -522,11 +523,8 @@
             pltpu.VMEM((ITERS, groups, 1, 128), F32),
             pltpu.VMEM((ITERS, *block16), BF16),
             pltpu.VMEM((ITERS, NEAR, 1, 128), F32),
-            pltpu.VMEM((ITERS, 1, 128), F32),
-            pltpu.VMEM((ITERS, 1, 128), F32),
             pltpu.VMEM((traits, width), F32),
             pltpu.VMEM(block16, F32),
-            pltpu.VMEM(block16, BF16),
             pltpu.VMEM(block16, F32),
             pltpu.VMEM((ITERS, 2, traits, rows), F32),
             pltpu.VMEM((ITERS, 2, traits, rows), F32),
@@ -536,17 +534,19 @@
             pltpu.VMEM((2, traits, rows), F32),
             pltpu.VMEM((chips, 1, 128), F32),
             pltpu.VMEM(block16, F32),
-            pltpu.VMEM(block16, BF16),
-            pltpu.VMEM((6, traits, 128), F32),
+            pltpu.VMEM(block16, F32),
+            pltpu.VMEM((7, traits, 128), F32),
             pltpu.SemaphoreType.DMA((23,)),
             pltpu.SemaphoreType.DMA((5,)),
             pltpu.SemaphoreType.DMA((6,)),
             pltpu.SemaphoreType.DMA((6,)),
-            pltpu.SemaphoreType.DMA((ITERS, 16)),
-            pltpu.SemaphoreType.DMA((ITERS, 16)),
+            pltpu.SemaphoreType.DMA((ITERS, 15)),
+            pltpu.SemaphoreType.DMA((ITERS, 15)),
         ],
         compiler_params=pltpu.CompilerParams(
-            collective_id=0, has_side_effects=True, vmem_limit_bytes=64 * 1024 * 1000
+            collective_id=0, has_side_effects=True, vmem_limit_bytes=64 * 1000 * 1000
+
+
         ),
     )(geno, resid, npeople, ncoef, coef, block, prior, sigma, gamma, counts)
 

time: 161 us -> 153 us (0.950); the launches traced: 161 us -> 151 us
  Pallas kernels: 156 us -> 146 us
    pallas_call x1, Pallas kernels: 156 us -> 146 us  [update(): pl.pallas_call(functools.partial(kernel, chips), name='gibbs', out_shape=...]
where the time goes in v3:
time: 153 us; the launch traced here: 151 us
  Pallas kernels  146 us (95%)
  local copies, waits for them, and re-layouts  3.97 us (3%)
    pallas_call x1, Pallas kernels, update(): pl.pallas_call(functools.partial(kernel, chips), name='gibbs', out_shape=...  146 us

profile of v3, /device:TPU:37, one launch (start us, length us, event | category | flops | bytes accessed | tf_op | source)
XLA Modules:
  0.0 151.5 jit_solution(11483130996683675323)
XLA Ops:
  1.3 146.2 %gibbs.1 = (f32[32,8192]{1,0:T(8,128)}, f32[32,256]{1,0:T(8,128)}, f32[1,128]{1,0:T(1,128)}) custom-call(bf16[256,4096]{1,0:T(8,128)(2,1)} %geno.1, f32[32,256]{1,0:T(8,128)} %resid.1, f32[32,256]{1,0:T(8,128)} %npeople.1, f32[32,4096]{1,0:T(8,128)} %ncoef.1, f32[32,8192]{1,0:T(8,128)} %coef.1, s32[1]{0:T(128)S(6)} %copy.15.block, f32[32]{0:T(128)} %prior.1, ...), custom_call_target="tpu_custom_call" | custom-call | tf_op jit(solution)/shard_map/gibbs/pallas_call | solution.py:492
  147.5 0.0 copy-start
  147.5 1.1 slice_bitcast_fusion
  148.6 2.3 %copy.16 = f32[32,8192]{1,0:T(8,128)} copy(f32[32,8192]{1,0:T(8,128)} %get-tuple-element.12) | data formatting | bytes 2097152
  150.9 0.0 copy-done
  150.9 0.6 copy.17
Async XLA Ops:
  147.5 3.4 %copy-start = (f32[32,256]{1,0:T(8,128)S(1)}, f32[32,256]{1,0:T(8,128)}, u32[]{:S(2)}) copy-start(f32[32,256]{1,0:T(8,128)} %get-tuple-element.13) | copy-start | bytes 98308

commit v4 on v3

--- a/solution.py
+++ b/solution.py
@@ -102,10 +102,6 @@
     def piece_at(offset):
         return lax.rem(r + offset + NEAR, NEAR)
 
-    barrier = pltpu.get_barrier_semaphore()
-    for target in (*[chip(offset) for offset in (*ENDS, *FULL)], partner):
-        pl.semaphore_signal(barrier, inc=1, device_id=target, device_id_type=MESH)
-
     mine = pl.multiple_of(k * half, half)
     other = pl.multiple_of((1 - k) * half, half)
     own_col = pl.multiple_of(k * half + r * width, width)
@@ -123,7 +119,6 @@
         loads.append(
             pltpu.make_async_copy(geno.at[:, pl.ds(at, width)], xh.at[0, piece], load_sem.at[7 + piece])
         )
-    for piece in range(NEAR):
         at = pl.multiple_of(other + piece * width, width)
         loads.append(
             pltpu.make_async_copy(geno.at[:, pl.ds(at, width)], xo.at[piece], load_sem.at[15 + piece])
@@ -137,6 +132,9 @@
     ]
     for copy in smalls + loads:
         copy.start()
+    barrier = pltpu.get_barrier_semaphore()
+    for target in (*[chip(offset) for offset in (*ENDS, *FULL)], partner):
+        pl.semaphore_signal(barrier, inc=1, device_id=target, device_id_type=MESH)
     for copy in smalls:
         copy.wait()
 
@@ -177,7 +175,8 @@
     def decoded(codes, unit):
         return codes.astype(jnp.int32).astype(F32) * unit
 
-    for copy in loads:
+    few = len(loads) - 2 * NEAR
+    for copy in loads[:few]:
         copy.wait()
     first = s_block[0] == 0
     old_mine = jnp.where(first, cf[0], cf[2]).astype(BF16)
@@ -185,6 +184,8 @@
     fitted_old = jnp.zeros((traits, rows), F32)
     for piece in range(NEAR):
         columns = slice(piece * width, (piece + 1) * width)
+        loads[few + 2 * piece].wait()
+        loads[few + 2 * piece + 1].wait()
         fitted_old += lax.dot_general(old_mine[:, columns], xh[0, piece], NT, preferred_element_type=F32)
         fitted_old += lax.dot_general(old_other[:, columns], xo[piece], NT, preferred_element_type=F32)
     partial_res = mask_own * (res[...] + fitted_old)
@@ -192,10 +193,6 @@
     target = (mask_own * (partial_res + jnp.sqrt(noise_var) * npl[...])).astype(BF16)
     for piece in range(NEAR):
         dsend[piece] = lax.dot_general(target, xo[piece], NN, preferred_element_type=F32)
-    for piece in range(NEAR):
-        dir_ref[piece] = lax.dot_general(target, xh[0, piece], NN, preferred_element_type=F32)
-    fitted[...] = jnp.zeros_like(fitted)
-    acc[...] = jnp.zeros_like(acc)
 
     pl.semaphore_wait(barrier, len(ENDS) + len(FULL) + 1)
 
@@ -215,6 +212,10 @@
     swap_sum.start()
     swap_res.start()
     swap_geno.start()
+    for piece in range(NEAR):
+        dir_ref[piece] = lax.dot_general(target, xh[0, piece], NN, preferred_element_type=F32)
+    fitted[...] = jnp.zeros_like(fitted)
+    acc[...] = jnp.zeros_like(acc)
     swap_sum.wait_recv()
 
     def send(src, dst, stage, number, target):
@@ -476,6 +477,10 @@
         return carry
 
     lax.fori_loop(0, ITERS, drain, 0)
+
+
+def loose(array):
+    return pltpu.with_memory_space_constraint(array, pltpu.HBM)
 
 
 def update(geno, resid, npeople, ncoef, coef, block, prior, sigma, gamma, counts):
@@ -544,11 +549,15 @@
             pltpu.SemaphoreType.DMA((ITERS, 15)),
         ],
         compiler_params=pltpu.CompilerParams(
-            collective_id=0, has_side_effects=True, vmem_limit_bytes=64 * 1000 * 1000
+            collective_id=0, has_side_effects=True, vmem_limit_bytes=40 * 1000 * 1000
 
 
         ),
-    )(geno, resid, npeople, ncoef, coef, block, prior, sigma, gamma, counts)
+    )(
+        *map(loose, (geno, resid, npeople, ncoef, coef)),
+        block,
+        *map(loose, (prior, sigma, gamma, counts)),
+    )
 
 
 def per_device(geno, resid, npeople, ncoef, coef, block, prior, sigma, gamma, counts):

time: 153 us -> 152 us (level)
  local copies, waits for them, and re-layouts: 3.97 us -> 2.1 us
where the time goes in v4:
time: 152 us; the launch traced here: 150 us
  Pallas kernels  147 us (97%)
  local copies, waits for them, and re-layouts  2.1 us (1%)
    pallas_call x1, Pallas kernels, update(): pl.pallas_call(functools.partial(kernel, chips), name='gibbs', out_shape=...  147 us

profile of v4, /device:TPU:37, one launch (start us, length us, event | category | flops | bytes accessed | tf_op | source)
XLA Modules:
  0.0 150.2 jit_solution(7205026836177995523)
XLA Ops:
  1.3 146.8 %gibbs.1 = (f32[32,8192]{1,0:T(8,128)S(1)}, f32[32,256]{1,0:T(8,128)S(1)}, f32[1,128]{1,0:T(1,128)S(1)}) custom-call(bf16[256,4096]{1,0:T(8,128)(2,1)} %geno.1, f32[32,256]{1,0:T(8,128)} %resid.1, f32[32,256]{1,0:T(8,128)} %npeople.1, f32[32,4096]{1,0:T(8,128)} %ncoef.1, f32[32,8192]{1,0:T(8,128)} %coef.1, s32[1]{0:T(128)S(6)} %copy.15.block, f32[32]{0:T(128)} %prior.1, ...), custom_call_target="tpu_custom_call" | custom-call | tf_op jit(solution)/shard_map/gibbs/pallas_call | solution.py:497
  148.1 0.5 slice_bitcast_fusion
  148.6 1.0 copy.16
  149.6 0.6 copy.17

commit v5 on v4

--- a/solution.py
+++ b/solution.py
@@ -96,8 +96,10 @@
     r = lax.rem(z, NEAR)
     partner = {AXIS: z * CORES + (1 - k)}
 
+    near = {o: {AXIS: lax.rem(z + o + chips, chips) * CORES + k} for o in (*ENDS, *FULL, NEAR, -NEAR)}
+
     def chip(offset):
-        return {AXIS: lax.rem(z + offset + chips, chips) * CORES + k}
+        return near.get(offset) or {AXIS: lax.rem(z + offset + chips, chips) * CORES + k}
 
     def piece_at(offset):
         return lax.rem(r + offset + NEAR, NEAR)
@@ -175,8 +177,7 @@
     def decoded(codes, unit):
         return codes.astype(jnp.int32).astype(F32) * unit
 
-    few = len(loads) - 2 * NEAR
-    for copy in loads[:few]:
+    for copy in loads:
         copy.wait()
     first = s_block[0] == 0
     old_mine = jnp.where(first, cf[0], cf[2]).astype(BF16)
@@ -184,8 +185,6 @@
     fitted_old = jnp.zeros((traits, rows), F32)
     for piece in range(NEAR):
         columns = slice(piece * width, (piece + 1) * width)
-        loads[few + 2 * piece].wait()
-        loads[few + 2 * piece + 1].wait()
         fitted_old += lax.dot_general(old_mine[:, columns], xh[0, piece], NT, preferred_element_type=F32)
         fitted_old += lax.dot_general(old_other[:, columns], xo[piece], NT, preferred_element_type=F32)
     partial_res = mask_own * (res[...] + fitted_old)
@@ -296,12 +295,11 @@
 
     def share(number, search, step):
         ag[number, r] = search.astype(BF16)
-        agn[number, r] = to_row([jnp.sum(search * search, axis=1, keepdims=True), step])
         for place, end in enumerate(ENDS):
             band = pl.ds(place * top, top)
             send(ag.at[number, r, band], ag.at[number, r, band], TAKE_OF[end], number, chip(end))
-            if place == 0:
-                send(agn.at[number, r], agn.at[number, r], 5, number, chip(end))
+        agn[number, r] = to_row([jnp.sum(search * search, axis=1, keepdims=True), step])
+        send(agn.at[number, r], agn.at[number, r], 5, number, chip(ENDS[0]))
         for offset in FULL:
             send(ag.at[number, r], ag.at[number, r], TAKE_OF[offset], number, chip(offset))
             send(agn.at[number, r], agn.at[number, r], 5, number, chip(offset))

time: 152 us -> 149 us (0.980); the launches traced: 150 us -> 149 us
  no operation moved by 1% of the time
where the time goes in v5:
time: 149 us
  Pallas kernels  146 us (98%)
  local copies, waits for them, and re-layouts  2.1 us (1%)
    pallas_call x1, Pallas kernels, update(): pl.pallas_call(functools.partial(kernel, chips), name='gibbs', out_shape=...  146 us

profile of v5, /device:TPU:37, one launch (start us, length us, event | category | flops | bytes accessed | tf_op | source)
XLA Modules:
  0.0 149.0 jit_solution(10934035323311107471)
XLA Ops:
  1.3 145.6 %gibbs.1 = (f32[32,8192]{1,0:T(8,128)S(1)}, f32[32,256]{1,0:T(8,128)S(1)}, f32[1,128]{1,0:T(1,128)S(1)}) custom-call(bf16[256,4096]{1,0:T(8,128)(2,1)} %geno.1, f32[32,256]{1,0:T(8,128)} %resid.1, f32[32,256]{1,0:T(8,128)} %npeople.1, f32[32,4096]{1,0:T(8,128)} %ncoef.1, f32[32,8192]{1,0:T(8,128)} %coef.1, s32[1]{0:T(128)S(6)} %copy.15.block, f32[32]{0:T(128)} %prior.1, ...), custom_call_target="tpu_custom_call" | custom-call | tf_op jit(solution)/shard_map/gibbs/pallas_call | solution.py:495
  146.9 0.5 slice_bitcast_fusion
  147.4 1.0 copy.16
  148.4 0.6 copy.17

commit v6 on v5

--- a/solution.py
+++ b/solution.py
@@ -210,7 +210,6 @@
     swap_geno = to_pair(xo, xh.at[1], 2)
     swap_sum.start()
     swap_res.start()
-    swap_geno.start()
     for piece in range(NEAR):
         dir_ref[piece] = lax.dot_general(target, xh[0, piece], NN, preferred_element_type=F32)
     fitted[...] = jnp.zeros_like(fitted)
@@ -230,7 +229,7 @@
     def arrived(ref, stage, number):
         pltpu.make_async_copy(ref, ref, st_recv.at[number, stage]).wait()
 
-    def sum_for_owner(number, part_of, column, relay, meanwhile=lambda: None):
+    def sum_for_owner(number, part_of, column, relay, meanwhile):
         for offsets in SENDS:
             pieces = [piece_at(offset) for offset in offsets]
             for offset, piece, part in zip(offsets, pieces, [part_of(piece) for piece in pieces]):
@@ -253,7 +252,6 @@
                     slot_id = FULL.index(offset)
                     send(line, cv_recv.at[number, slot_id], 1, number, chip(offset))
                     send(codes, rs_recv.at[number, slot_id], 0, number, chip(offset))
-        meanwhile()
         arrived(cv_recv.at[number], 1, number)
         sums = to_row([column])
         for slot_id in range(7):
@@ -277,6 +275,7 @@
             pass_on(g, 2 * NEAR, 10)
         pass_on(g, NEAR, 2)
         pass_on(g, -NEAR, 8)
+        meanwhile()
         arrived(mcv.at[number, 0], 9, number)
         arrived(mid.at[number, 0], 8, number)
         if relay:
@@ -358,7 +357,7 @@
         dir_ref[...] = ag[number].astype(F32) + vals[6][:, 0:1][None] * dir_ref[...]
 
     zero = jnp.zeros((traits, 1), F32)
-    total, _ = sum_for_owner(0, lambda piece: dir_ref[piece] + drecv[piece], zero, True)
+    total, _ = sum_for_owner(0, lambda piece: dir_ref[piece] + drecv[piece], zero, True, swap_geno.start)
     search = total / noise_var + jnp.sqrt(ridge) * nco[...]
     search_ref[...] = search
     share(0, search, zero)

time: 149 us -> 149 us (level)
  no operation moved by 1% of the time
where the time goes in v6:
time: 149 us
  Pallas kernels  146 us (98%)
  local copies, waits for them, and re-layouts  2.1 us (1%)
    pallas_call x1, Pallas kernels, update(): pl.pallas_call(functools.partial(kernel, chips), name='gibbs', out_shape=...  146 us

profile of v6, /device:TPU:37, one launch (start us, length us, event | category | flops | bytes accessed | tf_op | source)
XLA Modules:
  0.0 148.9 jit_solution(3881199003104602003)
XLA Ops:
  1.3 145.5 %gibbs.1 = (f32[32,8192]{1,0:T(8,128)S(1)}, f32[32,256]{1,0:T(8,128)S(1)}, f32[1,128]{1,0:T(1,128)S(1)}) custom-call(bf16[256,4096]{1,0:T(8,128)(2,1)} %geno.1, f32[32,256]{1,0:T(8,128)} %resid.1, f32[32,256]{1,0:T(8,128)} %npeople.1, f32[32,4096]{1,0:T(8,128)} %ncoef.1, f32[32,8192]{1,0:T(8,128)} %coef.1, s32[1]{0:T(128)S(6)} %copy.15.block, f32[32]{0:T(128)} %prior.1, ...), custom_call_target="tpu_custom_call" | custom-call | tf_op jit(solution)/shard_map/gibbs/pallas_call | solution.py:494
  146.8 0.5 slice_bitcast_fusion
  147.3 1.0 copy.16
  148.3 0.6 copy.17
